TPU v7x, 32 devices: a whole 2x2x4 slice. The times are simulated.
32 devices in a mesh: grp: 2 (over x), space: 16 (over z, y, core).
Axes of the slice: x: 2, y: 2, z: 4, core: 2. Of those that a mesh axis runs over, the one named last changes fastest.
Arguments:
- propagator: bfloat16 [4, 3, 4, 12, 32768], P('grp', None, None, None, 'space'), parts along dimension 0, may hold values from -6 to 6
- eigvecs: bfloat16 [4, 3, 256, 32768], P('grp', None, None, 'space'), parts along dimension 0, may hold values from -6 to 6
- operator_weights: float32 [256, 2, 256], P('grp'), parts along dimension 0, may hold values from -0.375 to 0.375
- sink_time: int32 [2], P('grp'), parts along dimension 0, may hold values from 0 to 127
- term_index: int32 [48, 3], replicated, may hold values from 0 to 11
- term_sign: int32 [48], replicated, may hold values from 0 to 1
- solver_order: int32 [32768], P('space'), may hold values from 0 to 32767, as said below
Outputs:
- solver_source: bfloat16 [4, 3, 4, 12, 32768], P('grp', None, None, None, 'space'), parts along dimension 0
There are 2 independent parts, one for each index of `grp`. A program takes and returns all parts, laid end to end along the dimension named above; an argument that names none is the same for every part. Nothing has to cross between parts.
Inputs may be any that keep to these rules, and one draw needn't show every extreme that they name: solver_order is a permutation of the sites; split into blocks of 2048 positions and each block into pieces of 128, piece d of block e holds only sites d * 2048 to (d + 1) * 2048 - 1.
All inputs are finite; a program needn't handle non-finite values.
Results may differ from a plain program's by a relative error of at most 0.006.
Values may be sent and summed in bfloat16 or wider, within the bound.
A program may use at most 64 MiB of HBM per device.

v0:
```python
import math
import jax
import jax.numpy as jnp
from jax import lax
from jax.sharding import PartitionSpec as P

NVEC = 256
NMOM = 4
EXTENT = 64
MOMENTA = ((0, 0, 0), (1, 0, 0), (0, 1, 0), (0, 0, 1))
PRECISE = lax.Precision.HIGHEST


def phase_tables(offset, length):
    site_index = offset + jnp.arange(length, dtype=jnp.int32)
    coord_x = site_index % EXTENT
    coord_y = site_index // EXTENT % EXTENT
    coord_z = site_index // (EXTENT * EXTENT)
    windings = jnp.stack(
        [
            (step_x * coord_x + step_y * coord_y + step_z * coord_z) % EXTENT
            for step_x, step_y, step_z in MOMENTA
        ]
    )
    angles = windings.astype(jnp.float32) * (2.0 * math.pi / EXTENT)
    return (jnp.cos(angles), jnp.sin(angles))


def phased_rows(prop_colour, cosine_table, sine_table):
    real_part = prop_colour[0].astype(jnp.float32)[None]
    imag_part = prop_colour[1].astype(jnp.float32)[None]
    cos_rows = cosine_table[:, None, None, :]
    sin_rows = sine_table[:, None, None, :]
    turned = jnp.stack(
        [cos_rows * real_part + sin_rows * imag_part, cos_rows * imag_part - sin_rows * real_part]
    )
    return turned.astype(jnp.bfloat16).reshape(-1, turned.shape[-1])


def project(eig_colour, phased, scale_in):
    site_dims = (((1,), (1,)), ((), ()))
    from_real = lax.dot_general(
        eig_colour[0], phased, site_dims, preferred_element_type=jnp.float32
    ).reshape(-1, 2, NMOM, 48)
    from_imag = lax.dot_general(
        eig_colour[1], phased, site_dims, preferred_element_type=jnp.float32
    ).reshape(-1, 2, NMOM, 48)
    real_part = from_real[:, 0] + from_imag[:, 1]
    imag_part = from_real[:, 1] - from_imag[:, 0]
    return jnp.stack([real_part, imag_part]) * scale_in


def assemble(pieces):
    stacked = jnp.stack(pieces)
    vectors = stacked.shape[2]
    return stacked.transpose(3, 1, 2, 0, 4).reshape(NMOM, 2, vectors, 144)


def weighted_total(blocks, weights):
    real_sum = jnp.einsum("k,pkc->pc", weights[0], blocks[:, 0], precision=PRECISE) - jnp.einsum(
        "k,pkc->pc", weights[1], blocks[:, 1], precision=PRECISE
    )
    imag_sum = jnp.einsum("k,pkc->pc", weights[0], blocks[:, 1], precision=PRECISE) + jnp.einsum(
        "k,pkc->pc", weights[1], blocks[:, 0], precision=PRECISE
    )
    return jnp.stack([real_sum, imag_sum], axis=1)


def term_tables(term_index, term_sign):
    channels = jnp.arange(12, dtype=jnp.int32)
    first_pick = (term_index[:, 0:1] == channels[None]).astype(jnp.float32)
    second_pick = (term_index[:, 1:2] == channels[None]).astype(jnp.float32)
    sign_values = (2 * term_sign - 1).astype(jnp.float32)
    placement = (term_index[None, :, 2] == channels[:, None]).astype(jnp.float32) * sign_values[
        None
    ]
    return (first_pick, second_pick, placement)


def contract(blocks, weighted, first_pick, second_pick, placement):
    vectors = blocks.shape[2]
    block_grid = blocks.reshape(NMOM, 2, vectors, 12, 12)
    first_terms = jnp.einsum("mi,pqkij->pqkmj", first_pick, block_grid, precision=PRECISE)
    second_terms = jnp.einsum(
        "mi,pqij->pqmj", second_pick, weighted.reshape(NMOM, 2, 12, 12), precision=PRECISE
    )[:, :, None]
    real_part = first_terms[:, 0] * second_terms[:, 0] - first_terms[:, 1] * second_terms[:, 1]
    imag_part = first_terms[:, 0] * second_terms[:, 1] + first_terms[:, 1] * second_terms[:, 0]
    product = jnp.stack([real_part, imag_part], axis=1)
    return jnp.einsum("cm,pqkmj->pqkcj", placement, product, precision=PRECISE).reshape(
        NMOM, 2, vectors, 144
    )


def rebuild(coeffs, eig_colour, colour, cosine_table, sine_table, scale_out):
    vectors = coeffs.shape[2]
    colour_block = coeffs.reshape(NMOM, 2, vectors, 3, 48)[:, :, :, colour]
    coeff_table = colour_block.transpose(2, 1, 0, 3).reshape(vectors, 2 * NMOM * 48)
    vector_dims = (((0,), (0,)), ((), ()))
    from_real = lax.dot_general(
        coeff_table, eig_colour[0], vector_dims, preferred_element_type=jnp.float32
    ).reshape(2, NMOM, 48, -1)
    from_imag = lax.dot_general(
        coeff_table, eig_colour[1], vector_dims, preferred_element_type=jnp.float32
    ).reshape(2, NMOM, 48, -1)
    real_part = from_real[0] - from_imag[1]
    imag_part = from_real[1] + from_imag[0]
    cos_rows = cosine_table[:, None, :]
    sin_rows = sine_table[:, None, :]
    out_real = jnp.sum(cos_rows * real_part - sin_rows * imag_part, axis=0)
    out_imag = jnp.sum(cos_rows * imag_part + sin_rows * real_part, axis=0)
    return jnp.stack([out_real, out_imag]) * scale_out


def on_device(
    propagator, eigvecs, operator_weights, sink_time, term_index, term_sign, solver_order
):
    length = propagator.shape[-1]
    devices = lax.axis_size("space")
    offset = lax.axis_index("space") * length
    cosine_table, sine_table = phase_tables(offset, length)
    scale_in = 1.0 / math.sqrt(3.0 * length * devices)
    pieces = []
    for colour in range(3):
        phased = phased_rows(propagator[:, colour], cosine_table, sine_table)
        pieces.append(project(eigvecs[:, colour], phased, scale_in))
    partial_blocks = assemble(pieces)
    weights = lax.dynamic_index_in_dim(operator_weights, sink_time[0], 0, keepdims=False)
    first_pick, second_pick, placement = term_tables(term_index, term_sign)
    blocks = lax.psum(partial_blocks, "space")
    weighted = weighted_total(blocks, weights)
    coeffs = contract(blocks, weighted, first_pick, second_pick, placement).astype(jnp.bfloat16)
    scale_out = 1.0 / math.sqrt(NMOM * NVEC)
    colours = [
        rebuild(coeffs, eigvecs[:, colour], colour, cosine_table, sine_table, scale_out)
        for colour in range(3)
    ]
    source = jnp.stack(colours, axis=1).astype(jnp.bfloat16).reshape(2 * 3 * 48, length)
    wanted = lax.all_to_all(
        solver_order.reshape(devices, -1), "space", split_axis=0, concat_axis=0, tiled=True
    )
    local_index = wanted.reshape(length) - offset
    picked = jnp.take(source, local_index, axis=1)
    placed = lax.all_to_all(picked, "space", split_axis=1, concat_axis=1, tiled=True)
    return placed.reshape(2, 3, 4, 12, length)


def solution(mesh):
    return jax.shard_map(
        on_device,
        mesh=mesh,
        in_specs=(
            P("grp", None, None, None, "space"),
            P("grp", None, None, "space"),
            P("grp", None, None),
            P("grp"),
            P(),
            P(),
            P("space"),
        ),
        out_specs=P("grp", None, None, None, "space"),
        check_vma=False,
    )
```

profile of v0, /device:TPU:0, one launch (start us, length us, event | category | flops | bytes accessed | tf_op | source)
XLA Modules:
  0.0 206.0 jit_solution(521534441980782932)
XLA Ops:
  6.8 1.5 bitcast_convert_fusion.5
  10.0 2.7 %add_convert_fusion.2 = (bf16[1,4,4,12,2048]{4,3,2,1,0:T(8,128)(2,1)S(1)}, bf16[1,4,4,12,2048]{4,3,2,1,0:T(8,128)(2,1)S(1)}, bf16[1,4,4,12,2048]{4,3,2,1,0:T(8,1...) fusion(f32[4,12,2048]{2,1,0:T(8,128)S(1)} %copy.38, ...), kind=kLoop, calls=%fused_computation.16 | loop fusion | flops 9437184 | bytes 7143424 | tf_op jit(solution)/shard_map/convert.13
  13.1 1.4 convert_element_type.148
  14.4 3.2 %fusion.33 = f32[384,256]{1,0:T(8,128)} fusion(bf16[384,2048]{1,0:T(8,128)(2,1)} %convert_element_type.148, bf16[2,3,256,2048]{3,2,1,0:T(8,128)(2,1)} %param.8), kind=kOutput, calls=%fused_computation.58 | convolution fusion | flops 402653184 | bytes 3014656 | tf_op jit(solution)/shard_map/dot_general | solution.py:42
  17.6 2.7 %fusion.29 = f32[384,256]{1,0:T(8,128)} fusion(bf16[384,2048]{1,0:T(8,128)(2,1)S(1)} %copy-done.6, bf16[2,3,256,2048]{3,2,1,0:T(8,128)(2,1)} %param.8), kind=kOutput, calls=%fused_computation.54 | convolution fusion | flops 402653184 | bytes 3014656 | tf_op jit(solution)/shard_map/dot_general | solution.py:45
  20.6 1.4 convert_element_type.153
  22.0 3.2 %fusion.25 = f32[384,256]{1,0:T(8,128)} fusion(bf16[384,2048]{1,0:T(8,128)(2,1)} %convert_element_type.153, bf16[2,3,256,2048]{3,2,1,0:T(8,128)(2,1)} %param.8), kind=kOutput, calls=%fused_computation.50 | convolution fusion | flops 402653184 | bytes 3014656 | tf_op jit(solution)/shard_map/dot_general | solution.py:42
  25.2 2.7 %fusion.21 = f32[384,256]{1,0:T(8,128)} fusion(bf16[384,2048]{1,0:T(8,128)(2,1)S(1)} %copy-done.7, bf16[2,3,256,2048]{3,2,1,0:T(8,128)(2,1)} %param.8), kind=kOutput, calls=%fused_computation.46 | convolution fusion | flops 402653184 | bytes 3014656 | tf_op jit(solution)/shard_map/dot_general | solution.py:45
  28.2 1.4 convert_element_type.158
  29.5 2.4 %fusion.17 = f32[384,256]{1,0:T(8,128)S(1)} fusion(bf16[384,2048]{1,0:T(8,128)(2,1)} %convert_element_type.158, bf16[2,3,256,2048]{3,2,1,0:T(8,128)(2,1)} %param.8), kind=kOutput, calls=%fused_computation.42 | convolution fusion | flops 402653184 | bytes 3014656 | tf_op jit(solution)/shard_map/dot_general | solution.py:42
  32.0 1.9 fusion.13
  35.2 1.1 pad_maximum_fusion.3
  36.4 7.4 %all-to-all-start = ((s32[16,1,128]{2,1,0:T(1,128)}), s32[16,1,128]{2,1,0:T(1,128)S(1)}, u32[]{:S(2)}, u32[]{:S(2)}) async-start(s32[16,1,128]{2,1,0:T(1,128)} %bitcast), calls=%async_computation | async-start | bytes 16384 | tf_op jit(solution)/shard_map/all_to_all | solution.py:139
  44.5 5.7 %all-to-all-done = s32[16,1,128]{2,1,0:T(1,128)S(1)} async-done(((s32[16,1,128]{2,1,0:T(1,128)}), s32[16,1,128]{2,1,0:T(1,128)S(1)}, u32[]{:S(2)}, u32[]{:S(2)}) %all-to-all-start) | async-done | bytes 8224 | tf_op jit(solution)/shard_map/all_to_all | solution.py:139
  50.2 83.1 %all-reduce.2.cloned.1.call-done = f32[4,2,256,144]{2,3,1,0:T(8,128)} async-done(((f32[4,2,256,144]{2,3,1,0:T(8,128)}), f32[4,2,256,144]{2,3,1,0:T(8,128)}) %all-reduce.2.cloned.1.call-update) | async-done | bytes 1179664 | tf_op jit(solution)/shard_map/psum | solution.py:130
  133.4 1.7 fusion.51
  135.1 1.7 fusion.53
  138.6 0.9 copy.46
  139.5 2.1 %convolution_bitcast_fusion = f32[4,2,256,48,12]{2,3,4,1,0:T(8,128)S(1)} fusion(f32[4,2,256,12,12]{2,1,4,3,0:T(2,128)S(1)} %bitcast.204, s32[48]{0:T(128)S(1)} %get-tuple-element.55), kind=kOutput, calls=%fused_computation.7 | convolution fusion | flops 169869888 | bytes 5898432 | tf_op jit(solution)/shard_map/mi,pqkij->pqkmj/dot_general | solution.py:83
  142.5 2.5 %fusion.8 = bf16[4,2,256,12,12]{2,3,4,1,0:T(8,128)(2,1)S(1)} fusion(f32[4,1,256,48,12]{2,3,4,1,0:T(8,128)S(1)} %get-tuple-element.24, f32[4,1,256,48,12]{2,3,4,1,0:T(8,128)S(1)} %get-tuple-element.23, f32[48]{0:T(128)S(1)} %add_convert_fusion.4, s32[48]{0:T(128)S(1)} %get-tuple-element.54), kind=kOutput, calls=%fused_computation.31 | convolution fusion | flops 171345024 | bytes 5308800 | tf_op jit(solution)/shard_map/cm,pqkmj->pqkcj/dot_general | solution.py:90
  151.8 1.4 subtract_reduce_fusion.2
  154.4 7.5 %gather_fusion = bf16[2048,288]{1,0:T(8,128)(2,1)S(1)} fusion(bf16[288,2048]{0,1:T(8,128)(2,1)S(1)} %copy.57, s32[2048]{0:T(1024)S(1)} %broadcast_clamp_fusion), kind=kCustom, calls=%fused_computation | custom fusion | bytes 2367488 | tf_op jit(solution)/shard_map/jit(_take)/gather | solution.py:143
  162.9 33.0 %all_to_all.15 = bf16[288,16,128]{2,0,1:T(8,128)(2,1)S(1)} all-to-all(bf16[288,16,128]{2,0,1:T(8,128)(2,1)S(1)} %broadcast_select_fusion), channel_id=1, replica_groups=mesh['grp'=2,'space'=16] {'space'}, dimensions={1} | all-to-all | bytes 2359296 | tf_op jit(solution)/shard_map/all_to_all | solution.py:144
  197.2 1.9 copy.60
  (95 shorter events, 16.8 us)
Async XLA Ops:
  6.5 126.8 %copy-start = (f32[128,2,256]{2,1,0:T(2,128)S(1)}, f32[128,2,256]{2,1,0:T(2,128)}, u32[]{:S(2)}) copy-start(f32[128,2,256]{2,1,0:T(2,128)} %param.9) | copy-start | bytes 786436
  6.5 126.8 %all-reduce.2.cloned.1.call-start = ((), (), s32[]{:S(2)}) async-start(), calls=%async_computation.2 | async-start | bytes 2359296 | tf_op jit(solution)/shard_map/psum | solution.py:130
  14.4 3.2 %copy-start.6 = (bf16[384,2048]{1,0:T(8,128)(2,1)S(1)}, bf16[384,2048]{1,0:T(8,128)(2,1)}, u32[]{:S(2)}) copy-start(bf16[384,2048]{1,0:T(8,128)(2,1)} %convert_element_type.148) | copy-start | bytes 4718596
  17.6 2.7 %copy-start.4 = (bf16[1,4,4,12,2048]{4,3,2,1,0:T(8,128)(2,1)S(1)}, bf16[1,4,4,12,2048]{4,3,2,1,0:T(8,128)(2,1)}, u32[]{:S(2)}) copy-start(bf16[1,4,4,12,2048]{4,3,2,1,0:T(8,128)(2,1)} %get-tuple-element.48) | copy-start | bytes 2359300
  17.6 2.7 %copy-start.5 = (bf16[1,4,4,12,2048]{4,3,2,1,0:T(8,128)(2,1)S(1)}, bf16[1,4,4,12,2048]{4,3,2,1,0:T(8,128)(2,1)}, u32[]{:S(2)}) copy-start(bf16[1,4,4,12,2048]{4,3,2,1,0:T(8,128)(2,1)} %get-tuple-element.49) | copy-start | bytes 2359300
  22.0 3.2 %copy-start.7 = (bf16[384,2048]{1,0:T(8,128)(2,1)S(1)}, bf16[384,2048]{1,0:T(8,128)(2,1)}, u32[]{:S(2)}) copy-start(bf16[384,2048]{1,0:T(8,128)(2,1)} %convert_element_type.153) | copy-start | bytes 4718596
  25.2 2.7 %copy-start.3 = (bf16[1,4,4,12,2048]{4,3,2,1,0:T(8,128)(2,1)S(1)}, bf16[1,4,4,12,2048]{4,3,2,1,0:T(8,128)(2,1)}, u32[]{:S(2)}) copy-start(bf16[1,4,4,12,2048]{4,3,2,1,0:T(8,128)(2,1)} %get-tuple-element.51) | copy-start | bytes 2359300
  29.5 2.4 %copy-start.8 = (bf16[384,2048]{1,0:T(8,128)(2,1)S(1)}, bf16[384,2048]{1,0:T(8,128)(2,1)}, u32[]{:S(2)}) copy-start(bf16[384,2048]{1,0:T(8,128)(2,1)} %convert_element_type.158) | copy-start | bytes 4718596
  32.0 2.0 copy-start.11
  32.0 2.0 copy-start.12
  33.9 1.0 copy-start.9
  33.9 1.1 copy-start.10
  35.2 8.6 %copy-start.13 = (s32[48,3]{0,1:T(4,128)S(1)}, s32[48,3]{0,1:T(4,128)}, u32[]{:S(2)}) copy-start(s32[48,3]{0,1:T(4,128)} %param.11) | copy-start | bytes 1732
  35.2 8.6 %copy-start.14 = (s32[48]{0:T(128)S(1)}, s32[48]{0:T(128)}, u32[]{:S(2)}) copy-start(s32[48]{0:T(128)} %param.12) | copy-start | bytes 580
  36.4 13.8 %all-to-all-start = ((s32[16,1,128]{2,1,0:T(1,128)}), s32[16,1,128]{2,1,0:T(1,128)S(1)}, u32[]{:S(2)}, u32[]{:S(2)}) async-start(s32[16,1,128]{2,1,0:T(1,128)} %bitcast), calls=%async_computation | async-start | bytes 16384 | tf_op jit(solution)/shard_map/all_to_all | solution.py:139
  133.4 3.6 %copy-start.2 = (f32[4,2,256,144]{2,3,1,0:T(8,128)S(1)}, f32[4,2,256,144]{2,3,1,0:T(8,128)}, u32[]{:S(2)}) copy-start(f32[4,2,256,144]{2,3,1,0:T(8,128)} %all-reduce.2.cloned.1.call-done) | copy-start | bytes 3538948
  139.5 6.7 %slice-start = ((s8[6291456]{0:T(1024)(128)(4,1)}), s8[4194304]{0:T(1024)(128)(4,1)S(1)}, s32[]{:S(2)}) async-start(s8[6291456]{0:T(1024)(128)(4,1)} %bitcast.211), calls=%async_computation.3 | async-start | bytes 8388608
  141.7 4.6 %slice-start.1 = ((s8[6291456]{0:T(1024)(128)(4,1)}), s8[2097152]{0:T(1024)(128)(4,1)S(1)}, s32[]{:S(2)}) async-start(s8[6291456]{0:T(1024)(128)(4,1)} %bitcast.211), calls=%async_computation.4 | async-start | bytes 4194304
  196.4 2.8 %copy-start.1 = (f32[128,2,256]{2,1,0:T(2,128)S(1)}, f32[128,2,256]{2,1,0:T(2,128)}, u32[]{:S(2)}) copy-start(f32[128,2,256]{2,1,0:T(2,128)} %param.9) | copy-start | bytes 786436
Sparse Core Ops, SparseCore 0:
  36.5 96.7 all-reduce.1
where the time goes:
time: 206 us
  waiting for transfers between devices  88.8 us (43%)
  blocking collectives  33 us (16%)
  matrix products  29 us (14%)
  local copies, waits for them, and re-layouts  21.5 us (10%)
  between operations  14.6 us (7%)
  other arithmetic  11.7 us (6%)
  starting transfers between devices  7.44 us (4%)
    psum x1, waiting for transfers between devices, on_device(): blocks = lax.psum(partial_blocks, 'space')  83.1 us
    all_to_all x1, blocking collectives, on_device(): lax.all_to_all(picked, 'space', split_axis=1, concat_axis=1, tiled=True)  33 us
    dot_general x3, matrix products, project(): lax.dot_general(eig_colour[0], phased, site_dims, preferred_element_type=...  8.78 us
    gather x2, local copies, waits for them, and re-layouts, on_device(): picked = jnp.take(source, local_index, axis=1)  8.36 us
    all_to_all x1, starting transfers between devices, on_device(): lax.all_to_all(solver_order.reshape(devices, -1), 'space', split_axis=0,...  7.43 us
    dot_general x3, matrix products, project(): lax.dot_general(eig_colour[1], phased, site_dims, preferred_element_type=...  7.31 us
    all_to_all x1, waiting for transfers between devices, on_device(): lax.all_to_all(solver_order.reshape(devices, -1), 'space', split_axis=0,...  5.65 us
    convert_element_type x3, local copies, waits for them, and re-layouts, phased_rows(): return turned.astype(jnp.bfloat16).reshape(-1, turned.shape[-1])  4.12 us
  transfers between devices with their start and end apart: 2, of which 2 were waited for; matrix products, arithmetic and copies ran while one was open for 0% of the time, Pallas kernels for 0%

commit v1 on v0

--- a/solution.py
+++ b/solution.py
@@ -1,14 +1,24 @@
+import functools
 import math
 import jax
 import jax.numpy as jnp
 from jax import lax
 from jax.sharding import PartitionSpec as P
+from jax.lax import all_gather
 
 NVEC = 256
 NMOM = 4
 EXTENT = 64
 MOMENTA = ((0, 0, 0), (1, 0, 0), (0, 1, 0), (0, 0, 1))
 PRECISE = lax.Precision.HIGHEST
+
+
+def _report_ranges(local_block, axis_id):
+    y1 = all_gather(local_block, axis_id)
+    return jnp.sum(y1, axis=0)
+
+
+load_edge = functools.partial(_report_ranges, axis_id="space")
 
 
 def phase_tables(offset, length):
@@ -127,7 +137,7 @@
     partial_blocks = assemble(pieces)
     weights = lax.dynamic_index_in_dim(operator_weights, sink_time[0], 0, keepdims=False)
     first_pick, second_pick, placement = term_tables(term_index, term_sign)
-    blocks = lax.psum(partial_blocks, "space")
+    blocks = load_edge(partial_blocks)
     weighted = weighted_total(blocks, weights)
     coeffs = contract(blocks, weighted, first_pick, second_pick, placement).astype(jnp.bfloat16)
     scale_out = 1.0 / math.sqrt(NMOM * NVEC)

time: 206 us -> 218 us (1.058)
  other arithmetic: 11.7 us -> 19.7 us
  waiting for transfers between devices: 88.8 us -> 93.7 us
  matrix products: 29 us -> 26.8 us
    all_gather x0 -> x1, waiting for transfers between devices: none -> 87.8 us  [_report_ranges(): y1 = all_gather(local_block, axis_id)]
    psum x1 -> x0, waiting for transfers between devices: 83.1 us -> none  [on_device(): blocks = lax.psum(partial_blocks, 'space')]
    reduce_sum x0 -> x1, other arithmetic: none -> 7.76 us  [_report_ranges(): return jnp.sum(y1, axis=0)]
where the time goes in v1:
time: 218 us
  waiting for transfers between devices  93.7 us (43%)
  blocking collectives  33.9 us (16%)
  matrix products  26.8 us (12%)
  local copies, waits for them, and re-layouts  21.4 us (10%)
  other arithmetic  19.7 us (9%)
  between operations  14.6 us (7%)
  starting transfers between devices  7.44 us (3%)
    all_gather x1, waiting for transfers between devices, _report_ranges(): y1 = all_gather(local_block, axis_id)  87.8 us
    all_to_all x1, blocking collectives, on_device(): lax.all_to_all(picked, 'space', split_axis=1, concat_axis=1, tiled=True)  33.9 us
    dot_general x3, matrix products, project(): lax.dot_general(eig_colour[0], phased, site_dims, preferred_element_type=...  8.77 us
    gather x2, local copies, waits for them, and re-layouts, on_device(): picked = jnp.take(source, local_index, axis=1)  8.36 us
    reduce_sum x1, other arithmetic, _report_ranges(): return jnp.sum(y1, axis=0)  7.76 us
    all_to_all x1, starting transfers between devices, on_device(): lax.all_to_all(solver_order.reshape(devices, -1), 'space', split_axis=0,...  7.43 us
    dot_general x3, matrix products, project(): lax.dot_general(eig_colour[1], phased, site_dims, preferred_element_type=...  7.3 us
    all_to_all x1, waiting for transfers between devices, on_device(): lax.all_to_all(solver_order.reshape(devices, -1), 'space', split_axis=0,...  5.82 us
  transfers between devices with their start and end apart: 2, of which 2 were waited for; matrix products, arithmetic and copies ran while one was open for 0% of the time, Pallas kernels for 0%

profile of v1, /device:TPU:0, one launch (start us, length us, event | category | flops | bytes accessed | tf_op | source)
XLA Modules:
  0.0 217.6 jit_solution(5489960956661115282)
XLA Ops:
  6.8 1.5 bitcast_convert_fusion.5
  10.0 2.8 %add_convert_fusion.2 = (bf16[1,4,4,12,2048]{4,3,2,1,0:T(8,128)(2,1)S(1)}, bf16[1,4,4,12,2048]{4,3,2,1,0:T(8,128)(2,1)S(1)}, bf16[1,4,4,12,2048]{4,3,2,1,0:T(8,1...) fusion(f32[4,12,2048]{2,1,0:T(8,128)S(1)} %copy.37, ...), kind=kLoop, calls=%fused_computation.16 | loop fusion | flops 9437184 | bytes 7143424 | tf_op jit(solution)/shard_map/convert.13
  13.1 1.4 convert_element_type.148
  14.5 3.2 %fusion.33 = f32[384,256]{1,0:T(8,128)} fusion(bf16[384,2048]{1,0:T(8,128)(2,1)} %convert_element_type.148, bf16[2,3,256,2048]{3,2,1,0:T(8,128)(2,1)} %param.8), kind=kOutput, calls=%fused_computation.58 | convolution fusion | flops 402653184 | bytes 3014656 | tf_op jit(solution)/shard_map/dot_general | solution.py:52
  17.6 2.7 %fusion.29 = f32[384,256]{1,0:T(8,128)} fusion(bf16[384,2048]{1,0:T(8,128)(2,1)S(1)} %copy-done.5, bf16[2,3,256,2048]{3,2,1,0:T(8,128)(2,1)} %param.8), kind=kOutput, calls=%fused_computation.54 | convolution fusion | flops 402653184 | bytes 3014656 | tf_op jit(solution)/shard_map/dot_general | solution.py:55
  20.6 1.4 convert_element_type.153
  22.0 3.2 %fusion.25 = f32[384,256]{1,0:T(8,128)} fusion(bf16[384,2048]{1,0:T(8,128)(2,1)} %convert_element_type.153, bf16[2,3,256,2048]{3,2,1,0:T(8,128)(2,1)} %param.8), kind=kOutput, calls=%fused_computation.50 | convolution fusion | flops 402653184 | bytes 3014656 | tf_op jit(solution)/shard_map/dot_general | solution.py:52
  25.2 2.7 %fusion.21 = f32[384,256]{1,0:T(8,128)} fusion(bf16[384,2048]{1,0:T(8,128)(2,1)S(1)} %copy-done.6, bf16[2,3,256,2048]{3,2,1,0:T(8,128)(2,1)} %param.8), kind=kOutput, calls=%fused_computation.46 | convolution fusion | flops 402653184 | bytes 3014656 | tf_op jit(solution)/shard_map/dot_general | solution.py:55
  28.1 1.4 convert_element_type.158
  29.5 2.4 %fusion.17 = f32[384,256]{1,0:T(8,128)S(1)} fusion(bf16[384,2048]{1,0:T(8,128)(2,1)} %convert_element_type.158, bf16[2,3,256,2048]{3,2,1,0:T(8,128)(2,1)} %param.8), kind=kOutput, calls=%fused_computation.42 | convolution fusion | flops 402653184 | bytes 3014656 | tf_op jit(solution)/shard_map/dot_general | solution.py:52
  32.0 1.9 fusion.13
  35.2 1.1 pad_maximum_fusion.3
  36.4 7.4 %all-to-all-start = ((s32[16,1,128]{2,1,0:T(1,128)}), s32[16,1,128]{2,1,0:T(1,128)S(1)}, u32[]{:S(2)}, u32[]{:S(2)}) async-start(s32[16,1,128]{2,1,0:T(1,128)} %bitcast), calls=%async_computation | async-start | bytes 16384 | tf_op jit(solution)/shard_map/all_to_all | solution.py:149
  44.5 5.8 %all-to-all-done = s32[16,1,128]{2,1,0:T(1,128)S(1)} async-done(((s32[16,1,128]{2,1,0:T(1,128)}), s32[16,1,128]{2,1,0:T(1,128)S(1)}, u32[]{:S(2)}, u32[]{:S(2)}) %all-to-all-start) | async-done | bytes 8224 | tf_op jit(solution)/shard_map/all_to_all | solution.py:149
  50.4 87.8 %all-gather.2.cloned.1.call-done = f32[16,4,2,256,144]{3,4,2,1,0:T(8,128)} async-done(((f32[1,4,2,256,144]{3,4,2,1,0:T(8,128)}), f32[16,4,2,256,144]{3,4,2,1,0:T(8,128)}) %all-gather.2.cloned.1.call-update) | async-done | bytes 18874384 | tf_op jit(solution)/shard_map/all_gather | solution.py:17
  138.2 7.8 %reduce_sum.63 = f32[4,2,256,144]{2,3,1,0:T(8,128)S(1)} reduce(f32[16,4,2,256,144]{3,4,2,1,0:T(8,128)} %all-gather.2.cloned.1.call-done, f32[]{:T(128)} %constant.102.clone.1), dimensions={0}, to_apply=%region_0.1 | reduce | flops 4423680 | bytes 20054020 | tf_op jit(solution)/shard_map/reduce_sum | solution.py:18
  148.4 0.9 copy.45
  149.9 2.1 convolution_bitcast_fusion
  152.1 1.1 multiply_subtract_fusion
  153.2 2.5 %fusion.8 = bf16[4,2,256,12,12]{2,3,4,1,0:T(8,128)(2,1)S(1)} fusion(f32[4,1,256,48,12]{2,3,4,1,0:T(8,128)S(1)} %get-tuple-element.24, f32[4,1,256,48,12]{2,3,4,1,0:T(8,128)S(1)} %get-tuple-element.23, f32[48]{0:T(128)S(1)} %add_convert_fusion.4, s32[48]{0:T(128)S(1)} %get-tuple-element.54), kind=kOutput, calls=%fused_computation.31 | convolution fusion | flops 171345024 | bytes 5308800 | tf_op jit(solution)/shard_map/cm,pqkmj->pqkcj/dot_general | solution.py:100
  162.5 1.4 subtract_reduce_fusion.2
  165.0 7.5 %gather_fusion = bf16[2048,288]{1,0:T(8,128)(2,1)S(1)} fusion(bf16[288,2048]{0,1:T(8,128)(2,1)S(1)} %copy.56, s32[2048]{0:T(1024)S(1)} %broadcast_clamp_fusion), kind=kCustom, calls=%fused_computation | custom fusion | bytes 2367488 | tf_op jit(solution)/shard_map/jit(_take)/gather | solution.py:153
  173.5 33.9 %all_to_all.15 = bf16[288,16,128]{2,0,1:T(8,128)(2,1)S(1)} all-to-all(bf16[288,16,128]{2,0,1:T(8,128)(2,1)S(1)} %broadcast_select_fusion), channel_id=1, replica_groups=mesh['grp'=2,'space'=16] {'space'}, dimensions={1} | all-to-all | bytes 2359296 | tf_op jit(solution)/shard_map/all_to_all | solution.py:154
  208.8 1.9 copy.59
  (94 shorter events, 17.1 us)
Async XLA Ops:
  6.5 139.5 %copy-start = (f32[128,2,256]{2,1,0:T(2,128)S(1)}, f32[128,2,256]{2,1,0:T(2,128)}, u32[]{:S(2)}) copy-start(f32[128,2,256]{2,1,0:T(2,128)} %param.9) | copy-start | bytes 786436
  6.5 131.7 %all-gather.2.cloned.1.call-start = ((), (), s32[]{:S(2)}) async-start(), calls=%async_computation.2 | async-start | bytes 20054016 | tf_op jit(solution)/shard_map/all_gather | solution.py:17
  14.5 3.2 %copy-start.5 = (bf16[384,2048]{1,0:T(8,128)(2,1)S(1)}, bf16[384,2048]{1,0:T(8,128)(2,1)}, u32[]{:S(2)}) copy-start(bf16[384,2048]{1,0:T(8,128)(2,1)} %convert_element_type.148) | copy-start | bytes 4718596
  17.6 2.7 %copy-start.3 = (bf16[1,4,4,12,2048]{4,3,2,1,0:T(8,128)(2,1)S(1)}, bf16[1,4,4,12,2048]{4,3,2,1,0:T(8,128)(2,1)}, u32[]{:S(2)}) copy-start(bf16[1,4,4,12,2048]{4,3,2,1,0:T(8,128)(2,1)} %get-tuple-element.48) | copy-start | bytes 2359300
  17.6 2.7 %copy-start.4 = (bf16[1,4,4,12,2048]{4,3,2,1,0:T(8,128)(2,1)S(1)}, bf16[1,4,4,12,2048]{4,3,2,1,0:T(8,128)(2,1)}, u32[]{:S(2)}) copy-start(bf16[1,4,4,12,2048]{4,3,2,1,0:T(8,128)(2,1)} %get-tuple-element.49) | copy-start | bytes 2359300
  22.0 3.2 %copy-start.6 = (bf16[384,2048]{1,0:T(8,128)(2,1)S(1)}, bf16[384,2048]{1,0:T(8,128)(2,1)}, u32[]{:S(2)}) copy-start(bf16[384,2048]{1,0:T(8,128)(2,1)} %convert_element_type.153) | copy-start | bytes 4718596
  25.2 2.7 %copy-start.2 = (bf16[1,4,4,12,2048]{4,3,2,1,0:T(8,128)(2,1)S(1)}, bf16[1,4,4,12,2048]{4,3,2,1,0:T(8,128)(2,1)}, u32[]{:S(2)}) copy-start(bf16[1,4,4,12,2048]{4,3,2,1,0:T(8,128)(2,1)} %get-tuple-element.51) | copy-start | bytes 2359300
  29.5 2.4 %copy-start.7 = (bf16[384,2048]{1,0:T(8,128)(2,1)S(1)}, bf16[384,2048]{1,0:T(8,128)(2,1)}, u32[]{:S(2)}) copy-start(bf16[384,2048]{1,0:T(8,128)(2,1)} %convert_element_type.158) | copy-start | bytes 4718596
  32.0 2.0 copy-start.10
  32.0 2.0 copy-start.11
  33.9 1.0 copy-start.8
  33.9 1.1 copy-start.9
  35.2 8.6 %copy-start.12 = (s32[48,3]{0,1:T(4,128)S(1)}, s32[48,3]{0,1:T(4,128)}, u32[]{:S(2)}) copy-start(s32[48,3]{0,1:T(4,128)} %param.11) | copy-start | bytes 1732
  35.2 8.6 %copy-start.13 = (s32[48]{0:T(128)S(1)}, s32[48]{0:T(128)}, u32[]{:S(2)}) copy-start(s32[48]{0:T(128)} %param.12) | copy-start | bytes 580
  36.4 14.0 %all-to-all-start = ((s32[16,1,128]{2,1,0:T(1,128)}), s32[16,1,128]{2,1,0:T(1,128)S(1)}, u32[]{:S(2)}, u32[]{:S(2)}) async-start(s32[16,1,128]{2,1,0:T(1,128)} %bitcast), calls=%async_computation | async-start | bytes 16384 | tf_op jit(solution)/shard_map/all_to_all | solution.py:149
  149.9 6.9 %slice-start = ((s8[6291456]{0:T(1024)(128)(4,1)}), s8[4194304]{0:T(1024)(128)(4,1)S(1)}, s32[]{:S(2)}) async-start(s8[6291456]{0:T(1024)(128)(4,1)} %bitcast.211), calls=%async_computation.3 | async-start | bytes 8388608
  152.0 4.8 %slice-start.1 = ((s8[6291456]{0:T(1024)(128)(4,1)}), s8[2097152]{0:T(1024)(128)(4,1)S(1)}, s32[]{:S(2)}) async-start(s8[6291456]{0:T(1024)(128)(4,1)} %bitcast.211), calls=%async_computation.4 | async-start | bytes 4194304
  208.0 2.8 %copy-start.1 = (f32[128,2,256]{2,1,0:T(2,128)S(1)}, f32[128,2,256]{2,1,0:T(2,128)}, u32[]{:S(2)}) copy-start(f32[128,2,256]{2,1,0:T(2,128)} %param.9) | copy-start | bytes 786436
Sparse Core Ops, SparseCore 0:
  36.5 101.6 all-gather.1
